TPU v7x, 32 devices: a whole 2x2x4 slice. The times are simulated.
32 devices in a mesh: wide: 8 (over z, y), narrow: 4 (over x, core).
Axes of the slice: x: 2, y: 2, z: 4, core: 2. Of those that a mesh axis runs over, the one named last changes fastest.
Arguments:
- layer_in: bfloat16 [8, 512, 1536], P('wide', 'narrow'), may hold values from -6 to 6
- lengths: int32 [8, 8], P('wide'), may hold values from 1 to 256, 512 in all within a row
- w_qkv: bfloat16 [1536, 2048], P(('wide', 'narrow')), may hold values from -0.15625 to 0.15625
- b_qkv: bfloat16 [2048], P(('wide', 'narrow')), may hold values from -3 to 3
- w_out: bfloat16 [1536, 1536], P(None, ('wide', 'narrow')), may hold values from -0.625 to 0.625
- norm1_gain: bfloat16 [1536], P(('wide', 'narrow')), may hold values from 0.099609375 to 1.8984375
- norm2_gain: bfloat16 [1536], P(('wide', 'narrow')), may hold values from 0.099609375 to 1.8984375
- w_gate: bfloat16 [1536, 8960], P('wide', 'narrow'), may hold values from -0.15625 to 0.15625
- w_up: bfloat16 [1536, 8960], P('wide', 'narrow'), may hold values from -0.15625 to 0.15625
- w_down: bfloat16 [8960, 1536], P('narrow', 'wide'), may hold values from -0.0625 to 0.0625
- grad_out: bfloat16 [8, 512, 1536], P('wide', 'narrow'), may hold values from -6 to 6
Outputs:
- layer_out: bfloat16 [8, 512, 1536], P('wide', 'narrow')
- grad_in: float32 [8, 512, 1536], P('wide', 'narrow')
- grad_w_qkv: float32 [1536, 2048], P(('wide', 'narrow'))
- grad_b_qkv: float32 [2048], P(('wide', 'narrow'))
- grad_w_out: float32 [1536, 1536], P(None, ('wide', 'narrow'))
- grad_norm1: float32 [1536], P(('wide', 'narrow'))
- grad_norm2: float32 [1536], P(('wide', 'narrow'))
- grad_w_gate: float32 [1536, 8960], P('wide', 'narrow')
- grad_w_up: float32 [1536, 8960], P('wide', 'narrow')
- grad_w_down: float32 [8960, 1536], P('narrow', 'wide')
Inputs may be any that keep to these rules, and one draw needn't show every extreme that they name: In each pack the 8 lengths sum to 512, and one of them is 256.
All inputs are finite; a program needn't handle non-finite values.
Results may differ from a plain program's by a relative error of at most 0.02.
Values may be sent and summed in bfloat16 or wider, within the bound.
A program may use at most 192 MiB of HBM per device.

v0:
```python
import math
import jax
import jax.numpy as jnp
from jax import lax
from jax.sharding import PartitionSpec as P

QUERY_HEADS = 12
KEY_VALUE_HEADS = 2
HEAD_WIDTH = 128
EPSILON = 1e-06
ROPE_BASE = 10000.0
NEGATIVE_BIG = -1e30
HIGHEST = lax.Precision.HIGHEST


def rms_scale(value_rows, gain):
    return (
        value_rows
        * lax.rsqrt(jnp.mean(value_rows * value_rows, axis=-1, keepdims=True) + EPSILON)
        * gain
    )


def apply_rotation(value_rows, token_position):
    half_dim = value_rows.shape[-1] // 2
    freq = jnp.exp(
        jnp.arange(half_dim, dtype=jnp.float32)
        * (-2.0 * math.log(ROPE_BASE) / value_rows.shape[-1])
    )
    angle = token_position[:, None] * freq[None, :]
    cosine = jnp.cos(angle)[:, None, :]
    sine = jnp.sin(angle)[:, None, :]
    leading = value_rows[..., :half_dim]
    trailing = value_rows[..., half_dim:]
    return jnp.concatenate(
        [leading * cosine - trailing * sine, trailing * cosine + leading * sine], axis=-1
    )


def doc_layout(index, doc_lengths):
    ends = jnp.cumsum(doc_lengths)
    starts = ends - doc_lengths
    document_index = jnp.sum((index[:, None] >= ends[None, :]).astype(jnp.int32), axis=1)
    onehot = (
        document_index[:, None] == jnp.arange(doc_lengths.shape[0], dtype=jnp.int32)[None, :]
    ).astype(jnp.int32)
    token_position = index - jnp.sum(onehot * starts[None, :], axis=1)
    return (document_index, token_position.astype(jnp.float32))


def contract_rows(left, right):
    return lax.dot_general(
        left, right, (((0,), (0,)), ((), ())), preferred_element_type=jnp.float32
    )


def times_transposed(left, right):
    return lax.dot_general(
        left, right, (((1,), (1,)), ((), ())), preferred_element_type=jnp.float32
    )


def shards(
    layer_in, lengths, w_qkv, b_qkv, w_out, norm1_gain, norm2_gain, w_gate, w_up, w_down, grad_out
):
    hidden_in = layer_in[0].astype(jnp.float32)
    rows_per_shard = hidden_in.shape[0]
    narrow_count = lax.axis_size("narrow")
    first_row = lax.axis_index("narrow") * rows_per_shard
    pack_rows = rows_per_shard * narrow_count
    query_group = QUERY_HEADS // KEY_VALUE_HEADS
    query_total_width = QUERY_HEADS * HEAD_WIDTH
    key_total_width = KEY_VALUE_HEADS * HEAD_WIDTH
    scale = HEAD_WIDTH ** (-0.5)
    doc_lengths = lengths[0]
    local_index = first_row + jnp.arange(rows_per_shard, dtype=jnp.int32)
    local_doc, local_pos = doc_layout(local_index, doc_lengths)
    key_index = jnp.arange(pack_rows, dtype=jnp.int32)
    key_doc = doc_layout(key_index, doc_lengths)[0]
    wqkv_full, bias_full, wout_full, gain_one, gain_two = (
        lax.all_gather(w_qkv, ("wide", "narrow"), axis=0, tiled=True),
        lax.all_gather(b_qkv, ("wide", "narrow"), axis=0, tiled=True),
        lax.all_gather(w_out, ("wide", "narrow"), axis=1, tiled=True),
        lax.all_gather(norm1_gain, ("wide", "narrow"), axis=0, tiled=True),
        lax.all_gather(norm2_gain, ("wide", "narrow"), axis=0, tiled=True),
    )
    wgate_full, wup_full, wdown_full = (
        lax.all_gather(w_gate, "wide", axis=0, tiled=True),
        lax.all_gather(w_up, "wide", axis=0, tiled=True),
        lax.all_gather(w_down, "wide", axis=1, tiled=True),
    )
    gain_one = gain_one.astype(jnp.float32)
    gain_two = gain_two.astype(jnp.float32)
    normed_one = rms_scale(hidden_in, gain_one).astype(jnp.bfloat16)
    unrotated_projection = jnp.dot(
        normed_one, wqkv_full, preferred_element_type=jnp.float32
    ) + bias_full.astype(jnp.float32)
    pre_query = unrotated_projection[:, :query_total_width].reshape(
        rows_per_shard, QUERY_HEADS, HEAD_WIDTH
    )
    unrotated_key = unrotated_projection[
        :, query_total_width : query_total_width + key_total_width
    ].reshape(rows_per_shard, KEY_VALUE_HEADS, HEAD_WIDTH)

    def rotate_local(value_rows):
        return apply_rotation(value_rows, local_pos)

    rotated_query, query_back = jax.vjp(rotate_local, pre_query)
    key_rot, key_backward = jax.vjp(rotate_local, unrotated_key)
    query_rows = rotated_query.astype(jnp.bfloat16).reshape(
        rows_per_shard, KEY_VALUE_HEADS, query_group, HEAD_WIDTH
    )
    key_local = key_rot.reshape(rows_per_shard, key_total_width).astype(jnp.bfloat16)
    value_local = unrotated_projection[:, query_total_width + key_total_width :].astype(
        jnp.bfloat16
    )
    every_key_row, every_value_row = (
        lax.all_gather(key_local, "narrow", axis=0, tiled=True),
        lax.all_gather(value_local, "narrow", axis=0, tiled=True),
    )
    rows_per_block = min(512, pack_rows)
    count_of_blocks = pack_rows // rows_per_block
    blocked_keys = every_key_row.reshape(
        count_of_blocks, rows_per_block, KEY_VALUE_HEADS, HEAD_WIDTH
    )
    blocked_values = every_value_row.reshape(
        count_of_blocks, rows_per_block, KEY_VALUE_HEADS, HEAD_WIDTH
    )
    doc_blocks = key_doc.reshape(count_of_blocks, rows_per_block)
    index_blocks = key_index.reshape(count_of_blocks, rows_per_block)
    input_per_block = (blocked_keys, blocked_values, doc_blocks, index_blocks)

    def block_scores(key_block, doc_block, index_block):
        scores = (
            jnp.einsum("tkgd,skd->kgts", query_rows, key_block, preferred_element_type=jnp.float32)
            * scale
        )
        allowed = (local_doc[:, None] == doc_block[None, :]) & (
            index_block[None, :] <= local_index[:, None]
        )
        return (jnp.where(allowed, scores, NEGATIVE_BIG), allowed)

    def total_block(carry, inputs):
        running_max, running_sum = carry
        key_block, value_block, doc_block, index_block = inputs
        masked, allowed = block_scores(key_block, doc_block, index_block)
        new_max = jnp.maximum(running_max, jnp.max(masked, axis=-1))
        probs = jnp.where(allowed, jnp.exp(masked - new_max[..., None]), 0.0)
        running_sum = running_sum * jnp.exp(running_max - new_max) + jnp.sum(probs, axis=-1)
        return ((new_max, running_sum), None)

    start_carry = (
        jnp.full((KEY_VALUE_HEADS, query_group, rows_per_shard), NEGATIVE_BIG, jnp.float32),
        jnp.zeros((KEY_VALUE_HEADS, query_group, rows_per_shard), jnp.float32),
    )
    (final_max, final_sum), _ = lax.scan(total_block, start_carry, input_per_block)
    log_total = final_max + jnp.log(final_sum)

    def block_probs(key_block, doc_block, index_block):
        masked, allowed = block_scores(key_block, doc_block, index_block)
        return jnp.where(allowed, jnp.exp(masked - log_total[..., None]), 0.0)

    def block_forward_pass(weighted, inputs):
        key_block, value_block, doc_block, index_block = inputs
        probs_low = block_probs(key_block, doc_block, index_block).astype(jnp.bfloat16)
        weighted = weighted + jnp.einsum(
            "kgts,skd->kgtd", probs_low, value_block, preferred_element_type=jnp.float32
        )
        return (weighted, None)

    attn_heads, _ = lax.scan(
        block_forward_pass,
        jnp.zeros((KEY_VALUE_HEADS, query_group, rows_per_shard, HEAD_WIDTH), jnp.float32),
        input_per_block,
    )
    attn_low = (
        attn_heads.transpose(2, 0, 1, 3)
        .reshape(rows_per_shard, query_total_width)
        .astype(jnp.bfloat16)
    )
    middle = hidden_in + jnp.dot(attn_low, wout_full, preferred_element_type=jnp.float32)
    normed_two = rms_scale(middle, gain_two).astype(jnp.bfloat16)
    pack_normed = lax.all_gather(normed_two, "narrow", axis=0, tiled=True)
    gate = jnp.dot(pack_normed, wgate_full, preferred_element_type=jnp.float32)
    up_part = jnp.dot(pack_normed, wup_full, preferred_element_type=jnp.float32)
    sigmoid_gate = jax.nn.sigmoid(gate)
    activated = gate * sigmoid_gate
    hidden_act = (activated * up_part).astype(jnp.bfloat16)
    mixed = lax.psum_scatter(
        jnp.dot(hidden_act, wdown_full, preferred_element_type=jnp.float32).astype(jnp.bfloat16),
        "narrow",
        scatter_dimension=0,
        tiled=True,
    ).astype(jnp.float32)
    layer_out = (middle + mixed).astype(jnp.bfloat16)
    wgate_back, wup_back, wdown_back = (
        lax.all_gather(w_gate, "wide", axis=0, tiled=True),
        lax.all_gather(w_up, "wide", axis=0, tiled=True),
        lax.all_gather(w_down, "wide", axis=1, tiled=True),
    )
    cotangent = grad_out[0]
    pack_cotangent = lax.all_gather(cotangent, "narrow", axis=0, tiled=True)
    grad_hidden = times_transposed(pack_cotangent, wdown_back)
    grad_wdown = contract_rows(hidden_act, pack_cotangent)
    grad_gate = (grad_hidden * up_part * sigmoid_gate * (1.0 + gate * (1.0 - sigmoid_gate))).astype(
        jnp.bfloat16
    )
    grad_up = (grad_hidden * activated).astype(jnp.bfloat16)
    grad_wgate = contract_rows(pack_normed, grad_gate)
    grad_wup = contract_rows(pack_normed, grad_up)
    grad_normed_two = lax.psum_scatter(
        (times_transposed(grad_gate, wgate_back) + times_transposed(grad_up, wup_back)).astype(
            jnp.bfloat16
        ),
        "narrow",
        scatter_dimension=0,
        tiled=True,
    ).astype(jnp.float32)
    norm_two_back = jax.vjp(rms_scale, middle, gain_two)[1]
    grad_middle_norm, grad_gain_two = norm_two_back(grad_normed_two)
    grad_middle = cotangent.astype(jnp.float32) + grad_middle_norm
    grad_attn_proj = grad_middle.astype(jnp.bfloat16)
    grad_wout = contract_rows(attn_low, grad_attn_proj)
    attention_gradient = times_transposed(grad_attn_proj, wout_full).astype(jnp.bfloat16)
    head_gradients = attention_gradient.reshape(
        rows_per_shard, KEY_VALUE_HEADS, query_group, HEAD_WIDTH
    )
    delta = jnp.einsum(
        "tkgd,kgtd->kgt", head_gradients.astype(jnp.float32), attn_heads, precision=HIGHEST
    )

    def block_backward_pass(grad_query, inputs):
        key_block, value_block, doc_block, index_block = inputs
        probs = block_probs(key_block, doc_block, index_block)
        grad_probs = jnp.einsum(
            "tkgd,skd->kgts", head_gradients, value_block, preferred_element_type=jnp.float32
        )
        grad_scores = (probs * (grad_probs - delta[..., None])).astype(jnp.bfloat16)
        grad_query = (
            grad_query
            + jnp.einsum(
                "kgts,skd->tkgd", grad_scores, key_block, preferred_element_type=jnp.float32
            )
            * scale
        )
        grad_key = (
            jnp.einsum(
                "kgts,tkgd->skd", grad_scores, query_rows, preferred_element_type=jnp.float32
            )
            * scale
        )
        grad_value = jnp.einsum(
            "kgts,tkgd->skd",
            probs.astype(jnp.bfloat16),
            head_gradients,
            preferred_element_type=jnp.float32,
        )
        return (grad_query, (grad_key, grad_value))

    grad_query, (grad_key_blocks, grad_value_blocks) = lax.scan(
        block_backward_pass,
        jnp.zeros((rows_per_shard, KEY_VALUE_HEADS, query_group, HEAD_WIDTH), jnp.float32),
        input_per_block,
    )
    local_key_gradients, grad_values_local = (
        lax.psum_scatter(
            grad_key_blocks.reshape(pack_rows, key_total_width).astype(jnp.bfloat16),
            "narrow",
            scatter_dimension=0,
            tiled=True,
        ).astype(jnp.float32),
        lax.psum_scatter(
            grad_value_blocks.reshape(pack_rows, key_total_width).astype(jnp.bfloat16),
            "narrow",
            scatter_dimension=0,
            tiled=True,
        ).astype(jnp.float32),
    )
    grad_pre_query = query_back(grad_query.reshape(rows_per_shard, QUERY_HEADS, HEAD_WIDTH))[0]
    unrotated_key_gradient = key_backward(
        local_key_gradients.reshape(rows_per_shard, KEY_VALUE_HEADS, HEAD_WIDTH)
    )[0]
    grad_pre = jnp.concatenate(
        [
            grad_pre_query.reshape(rows_per_shard, query_total_width),
            unrotated_key_gradient.reshape(rows_per_shard, key_total_width),
            grad_values_local,
        ],
        axis=1,
    ).astype(jnp.bfloat16)
    grad_bias = jnp.sum(grad_pre.astype(jnp.float32), axis=0)
    grad_wqkv = contract_rows(normed_one, grad_pre)
    grad_normed_one = times_transposed(grad_pre, wqkv_full)
    norm_one_back = jax.vjp(rms_scale, hidden_in, gain_one)[1]
    grad_input_norm, grad_gain_one = norm_one_back(grad_normed_one)
    grad_input = grad_middle + grad_input_norm
    sum_wqkv, sum_bias, sum_wout, sum_gain_one, sum_gain_two = (
        lax.psum_scatter(grad_wqkv, ("wide", "narrow"), scatter_dimension=0, tiled=True),
        lax.psum_scatter(grad_bias, ("wide", "narrow"), scatter_dimension=0, tiled=True),
        lax.psum_scatter(grad_wout, ("wide", "narrow"), scatter_dimension=1, tiled=True),
        lax.psum_scatter(grad_gain_one, ("wide", "narrow"), scatter_dimension=0, tiled=True),
        lax.psum_scatter(grad_gain_two, ("wide", "narrow"), scatter_dimension=0, tiled=True),
    )
    sum_wgate, sum_wup, sum_wdown = (
        lax.psum_scatter(
            grad_wgate.astype(jnp.bfloat16), "wide", scatter_dimension=0, tiled=True
        ).astype(jnp.float32),
        lax.psum_scatter(
            grad_wup.astype(jnp.bfloat16), "wide", scatter_dimension=0, tiled=True
        ).astype(jnp.float32),
        lax.psum_scatter(
            grad_wdown.astype(jnp.bfloat16), "wide", scatter_dimension=1, tiled=True
        ).astype(jnp.float32),
    )
    return (
        layer_out[None],
        grad_input[None],
        sum_wqkv,
        sum_bias,
        sum_wout,
        sum_gain_one,
        sum_gain_two,
        sum_wgate,
        sum_wup,
        sum_wdown,
    )


def solution(mesh):
    placed = (
        P("wide", "narrow", None),
        P("wide", None),
        P(("wide", "narrow"), None),
        P(("wide", "narrow")),
        P(None, ("wide", "narrow")),
        P(("wide", "narrow")),
        P(("wide", "narrow")),
        P("wide", "narrow"),
        P("wide", "narrow"),
        P("narrow", "wide"),
        P("wide", "narrow", None),
    )
    return jax.shard_map(
        shards,
        mesh=mesh,
        in_specs=placed,
        out_specs=(
            P("wide", "narrow", None),
            P("wide", "narrow", None),
            P(("wide", "narrow"), None),
            P(("wide", "narrow")),
            P(None, ("wide", "narrow")),
            P(("wide", "narrow")),
            P(("wide", "narrow")),
            P("wide", "narrow"),
            P("wide", "narrow"),
            P("narrow", "wide"),
        ),
        check_vma=False,
    )
```

profile of v0, /device:TPU:0, one launch (start us, length us, event | category | flops | bytes accessed | tf_op | source)
XLA Modules:
  0.0 1367.8 jit_solution(4092313823965801265)
XLA Ops:
  12.0 42.5 %all-reduce.11 = (bf16[2048]{0:T(1024)(128)(2,1)S(1)}, bf16[1536]{0:T(1024)(128)(2,1)S(1)}, bf16[1536]{0:T(1024)(128)(2,1)S(1)}) all-reduce(bf16[2048]{0:T(1024)(128)(2,1)S(1)} %dynamic-update-slice.1, bf16[1536]{0:T(1024)(128)(2,1)S(1)} %dynamic-update-slice, ...), channel_id=1, replica_groups=mesh['wide'=8,'narrow'=4] {'wide','narrow'}, use_global_device_ids=true, to_apply=%add.5 | all-reduce | flops 5120 | bytes 20480
  58.7 24.4 %all-gather.9.cloned.1.call-done = bf16[1536,2048]{1,0:T(8,128)(2,1)} async-done(((bf16[48,2048]{1,0:T(8,128)(2,1)}), bf16[1536,2048]{1,0:T(8,128)(2,1)}) %all-gather.9.cloned.1.call-update) | async-done | bytes 6291472 | tf_op jit(solution)/shard_map/all_gather | solution.py:81
  108.1 40.1 %all-gather.11.cloned.1.call-done = bf16[1536,1536]{0,1:T(8,128)(2,1)} async-done(((bf16[1536,48]{0,1:T(8,128)(2,1)}), bf16[1536,1536]{0,1:T(8,128)(2,1)}) %all-gather.11.cloned.1.call-update) | async-done | bytes 4718608 | tf_op jit(solution)/shard_map/all_gather | solution.py:83
  156.5 100.5 %all-gather.15.cloned.1.call-done = bf16[1536,2240]{1,0:T(8,128)(2,1)} async-done(((bf16[192,2240]{1,0:T(8,128)(2,1)}), bf16[1536,2240]{1,0:T(8,128)(2,1)}) %all-gather.15.cloned.1.call-update) | async-done | bytes 6881296 | tf_op jit(solution)/shard_map/all_gather | solution.py:88
  257.0 19.8 %all-gather.13.cloned.1.call-done = bf16[512,1536]{1,0:T(8,128)(2,1)} async-done(((bf16[128,1536]{1,0:T(8,128)(2,1)}), bf16[512,1536]{1,0:T(8,128)(2,1)}) %all-gather.13.cloned.1.call-update) | async-done | bytes 1572880 | tf_op jit(solution)/shard_map/all_gather | solution.py:183
  276.8 9.5 fusion.47
  286.3 100.9 %all-gather.17.cloned.1.call-done = bf16[1536,2240]{1,0:T(8,128)(2,1)} async-done(((bf16[192,2240]{1,0:T(8,128)(2,1)}), bf16[1536,2240]{1,0:T(8,128)(2,1)}) %all-gather.17.cloned.1.call-update) | async-done | bytes 6881296 | tf_op jit(solution)/shard_map/all_gather | solution.py:89
  387.2 9.3 fusion.48
  396.5 9.9 all-gather.21.cloned.1.call-done
  406.5 110.5 %all-gather.19.cloned.1.call-done = bf16[2240,1536]{0,1:T(8,128)(2,1)} async-done(((bf16[2240,192]{0,1:T(8,128)(2,1)}), bf16[2240,1536]{0,1:T(8,128)(2,1)}) %all-gather.19.cloned.1.call-update) | async-done | bytes 6881296 | tf_op jit(solution)/shard_map/all_gather | solution.py:90
  517.0 13.3 multiply_convert_fusion
  530.3 7.8 fusion.49
  543.3 8.8 convolution_convert_fusion.3
  552.5 17.1 %reduce-scatter.16.cloned.1.call-done = bf16[128,1536]{1,0:T(8,128)(2,1)} async-done(((bf16[512,1536]{1,0:T(8,128)(2,1)}), bf16[128,1536]{1,0:T(8,128)(2,1)}) %reduce-scatter.16.cloned.1.call-update) | async-done | bytes 393232 | tf_op jit(solution)/shard_map/reduce_scatter | solution.py:211
  572.8 27.9 %reduce-scatter.14.cloned.1.call-done = bf16[128,1536]{1,0:T(8,128)(2,1)} async-done(((bf16[512,1536]{1,0:T(8,128)(2,1)}), bf16[128,1536]{1,0:T(8,128)(2,1)}) %reduce-scatter.14.cloned.1.call-update) | async-done | bytes 393232 | tf_op jit(solution)/shard_map/reduce_scatter | solution.py:189
  622.7 8.9 convolution_convert_fusion.2
  633.1 7.6 convolution_convert_fusion.1
  642.1 7.5 convolution_convert_fusion
  674.3 43.1 %all-reduce.10 = (f32[2048]{0:T(1024)S(1)}, f32[1536]{0:T(1024)S(1)}, f32[1536]{0:T(1024)S(1)}) all-reduce(f32[2048]{0:T(1024)S(1)} %convert_reduce_fusion, f32[1536]{0:T(1024)S(1)} %get-tuple-element.83, f32[1536]{0:T(1024)S(1)} %copy-done.22), channel_id=8, replica_groups=mesh['wide'=8,'narrow'=4] {'wide','narrow'}, use_global_device_ids=true, to_apply=%region_16.17.clone | all-reduce | flops 5120 | bytes 40960
  720.3 75.0 %reduce-scatter.22.cloned.1.call-done = bf16[192,2240]{1,0:T(8,128)(2,1)} async-done(((bf16[1536,2240]{1,0:T(8,128)(2,1)}), bf16[192,2240]{1,0:T(8,128)(2,1)}) %reduce-scatter.22.cloned.1.call-update) | async-done | bytes 860176 | tf_op jit(solution)/shard_map/reduce_scatter | solution.py:305
  797.8 129.5 %reduce-scatter.24.cloned.1.call-done = bf16[192,2240]{1,0:T(8,128)(2,1)} async-done(((bf16[1536,2240]{1,0:T(8,128)(2,1)}), bf16[192,2240]{1,0:T(8,128)(2,1)}) %reduce-scatter.24.cloned.1.call-update) | async-done | bytes 860176 | tf_op jit(solution)/shard_map/reduce_scatter | solution.py:308
  929.8 129.4 %reduce-scatter.26.cloned.1.call-done = bf16[2240,192]{0,1:T(8,128)(2,1)} async-done(((bf16[2240,1536]{0,1:T(8,128)(2,1)}), bf16[2240,192]{0,1:T(8,128)(2,1)}) %reduce-scatter.26.cloned.1.call-update) | async-done | bytes 860176 | tf_op jit(solution)/shard_map/reduce_scatter | solution.py:311
  1061.6 139.1 %reduce-scatter.20.cloned.1.call-done = f32[1536,48]{0,1:T(8,128)} async-done(((f32[1536,1536]{0,1:T(8,128)}), f32[1536,48]{0,1:T(8,128)}) %reduce-scatter.20.cloned.1.call-update) | async-done | bytes 294928 | tf_op jit(solution)/shard_map/reduce_scatter | solution.py:300
  1200.8 160.3 %reduce-scatter.18.cloned.1.call-done = f32[48,2048]{1,0:T(8,128)} async-done(((f32[1536,2048]{1,0:T(8,128)}), f32[48,2048]{1,0:T(8,128)}) %reduce-scatter.18.cloned.1.call-update) | async-done | bytes 393232 | tf_op jit(solution)/shard_map/reduce_scatter | solution.py:298
  (191 shorter events, 110.2 us)
Async XLA Ops:
  7.2 75.9 %all-gather.9.cloned.1.call-start = ((), (), s32[]{:S(2)}) async-start(), calls=%async_computation.9 | async-start | bytes 6488064 | tf_op jit(solution)/shard_map/all_gather | solution.py:81
  7.9 140.3 %all-gather.11.cloned.1.call-start = ((), (), s32[]{:S(2)}) async-start(), calls=%async_computation.10 | async-start | bytes 4866048 | tf_op jit(solution)/shard_map/all_gather | solution.py:83
  8.7 248.4 %all-gather.15.cloned.1.call-start = ((), (), s32[]{:S(2)}) async-start(), calls=%async_computation.12 | async-start | bytes 7962624 | tf_op jit(solution)/shard_map/all_gather | solution.py:88
  9.4 267.4 %all-gather.13.cloned.1.call-start = ((), (), s32[]{:S(2)}) async-start(), calls=%async_computation.11 | async-start | bytes 1966080 | tf_op jit(solution)/shard_map/all_gather | solution.py:183
  56.5 31.0 %copy-start.12 = (f32[128,64]{1,0:T(8,128)}, f32[128,64]{1,0:T(8,128)S(1)}, u32[]{:S(2)}) copy-start(f32[128,64]{1,0:T(8,128)S(1)} %get-tuple-element.136) | copy-start | bytes 98308
  56.5 31.0 %copy-start.14 = (f32[128,64]{1,0:T(8,128)}, f32[128,64]{1,0:T(8,128)S(1)}, u32[]{:S(2)}) copy-start(f32[128,64]{1,0:T(8,128)S(1)} %get-tuple-element.137) | copy-start | bytes 98308
  56.6 31.5 %copy-start.17 = (f32[128,64]{0,1:T(8,128)}, f32[128,64]{0,1:T(8,128)S(1)}, u32[]{:S(2)}) copy-start(f32[128,64]{0,1:T(8,128)S(1)} %copy.113) | copy-start | bytes 98308
  56.7 31.4 %copy-start.19 = (f32[128,64]{0,1:T(8,128)}, f32[128,64]{0,1:T(8,128)S(1)}, u32[]{:S(2)}) copy-start(f32[128,64]{0,1:T(8,128)S(1)} %copy.114) | copy-start | bytes 98308
  57.9 25.2 %copy-start.28 = (f32[128]{0:T(128)}, f32[128]{0:T(128)S(1)}, u32[]{:S(2)}) copy-start(f32[128]{0:T(128)S(1)} %fusion.23) | copy-start | bytes 1540
  58.0 25.1 %copy-start.23 = (f32[128]{0:T(128)}, f32[128]{0:T(128)S(1)}, u32[]{:S(2)}) copy-start(f32[128]{0:T(128)S(1)} %fusion.36) | copy-start | bytes 1540
  105.5 42.6 %copy-start.3 = (bf16[1,128,1536]{2,1,0:T(8,128)(2,1)S(1)}, bf16[1,128,1536]{2,1,0:T(8,128)(2,1)}, u32[]{:S(2)}) copy-start(bf16[1,128,1536]{2,1,0:T(8,128)(2,1)} %param.11) | copy-start | bytes 1179652
  154.3 232.9 %all-gather.17.cloned.1.call-start = ((), (), s32[]{:S(2)}) async-start(), calls=%async_computation.13 | async-start | bytes 7962624 | tf_op jit(solution)/shard_map/all_gather | solution.py:89
  154.9 251.5 %all-gather.21.cloned.1.call-start = ((), (), s32[]{:S(2)}) async-start(), calls=%async_computation.22 | async-start | bytes 1966080 | tf_op jit(solution)/shard_map/all_gather | solution.py:202
  155.5 361.5 %all-gather.19.cloned.1.call-start = ((), (), s32[]{:S(2)}) async-start(), calls=%async_computation.14 | async-start | bytes 7962624 | tf_op jit(solution)/shard_map/all_gather | solution.py:90
  156.3 413.3 %reduce-scatter.16.cloned.1.call-start = ((), (), s32[]{:S(2)}) async-start(), calls=%async_computation.16 | async-start | bytes 1966080 | tf_op jit(solution)/shard_map/reduce_scatter | solution.py:211
  543.2 57.6 %reduce-scatter.14.cloned.1.call-start = ((), (), s32[]{:S(2)}) async-start(), calls=%async_computation.15 | async-start | bytes 1966080 | tf_op jit(solution)/shard_map/reduce_scatter | solution.py:189
  552.0 105.9 %reduce-scatter.28.cloned.1.call-start = ((), (), s32[]{:S(2)}) async-start(), calls=%async_computation.23 | async-start | bytes 327680
  618.2 43.4 %reduce-scatter.30.cloned.1.call-start = ((), (), s32[]{:S(2)}) async-start(), calls=%async_computation.24 | async-start | bytes 327680
  622.7 172.6 %reduce-scatter.22.cloned.1.call-start = ((), (), s32[]{:S(2)}) async-start(), calls=%async_computation.19 | async-start | bytes 7962624 | tf_op jit(solution)/shard_map/reduce_scatter | solution.py:305
  631.7 295.6 %reduce-scatter.24.cloned.1.call-start = ((), (), s32[]{:S(2)}) async-start(), calls=%async_computation.20 | async-start | bytes 7962624 | tf_op jit(solution)/shard_map/reduce_scatter | solution.py:308
  640.7 418.5 %reduce-scatter.26.cloned.1.call-start = ((), (), s32[]{:S(2)}) async-start(), calls=%async_computation.21 | async-start | bytes 7962624 | tf_op jit(solution)/shard_map/reduce_scatter | solution.py:311
  649.6 551.1 %reduce-scatter.20.cloned.1.call-start = ((), (), s32[]{:S(2)}) async-start(), calls=%async_computation.18 | async-start | bytes 9732096 | tf_op jit(solution)/shard_map/reduce_scatter | solution.py:300
  655.9 705.1 %reduce-scatter.18.cloned.1.call-start = ((), (), s32[]{:S(2)}) async-start(), calls=%async_computation.17 | async-start | bytes 12976128 | tf_op jit(solution)/shard_map/reduce_scatter | solution.py:298
  669.2 50.0 %copy-start.29 = (f32[128]{0:T(128)S(1)}, f32[128]{0:T(128)}, u32[]{:S(2)}) copy-start(f32[128]{0:T(128)} %copy-done.28) | copy-start | bytes 1540
  (28 other events, 98.0 us)
Sparse Core Ops, SparseCore 0:
  10.8 72.2 all-gather.8
  86.0 62.1 all-gather.10
  150.4 106.5 all-gather.14
  259.0 17.7 all-gather.12
  278.9 108.2 all-gather.16
  388.6 17.7 all-gather.20
  408.6 108.2 all-gather.18
  543.3 26.2 reduce-scatter.15
  572.7 28.0 reduce-scatter.13
  618.3 20.0 reduce-scatter.27
  641.4 20.0 reduce-scatter.29
  665.1 130.1 reduce-scatter.21
  799.0 128.2 reduce-scatter.23
  930.8 128.2 reduce-scatter.25
  1065.4 135.2 reduce-scatter.19
  1207.2 153.7 reduce-scatter.17
where the time goes:
time: 1380 us; the launch traced here: 1370 us
  waiting for transfers between devices  1090 us (79%)
  matrix products  117 us (8%)
  blocking collectives  97.3 us (7%)
  local copies, waits for them, and re-layouts  23.7 us (2%)
  other arithmetic  23 us (2%)
  between operations  14.7 us (1%)
    reduce_scatter x1, waiting for transfers between devices, shards(): lax.psum_scatter(grad_wqkv, ('wide', 'narrow'), scatter_dimension=0, tile...  160 us
    reduce_scatter x1, waiting for transfers between devices, shards(): lax.psum_scatter(grad_wout, ('wide', 'narrow'), scatter_dimension=1, tile...  139 us
    reduce_scatter x1, waiting for transfers between devices, shards(): lax.psum_scatter(grad_wup.astype(jnp.bfloat16), 'wide', scatter_dimension...  130 us
    reduce_scatter x1, waiting for transfers between devices, shards(): lax.psum_scatter(grad_wdown.astype(jnp.bfloat16), 'wide', scatter_dimensi...  129 us
    all_gather x1, waiting for transfers between devices, shards(): lax.all_gather(w_down, 'wide', axis=1, tiled=True)  111 us
    all_gather x1, waiting for transfers between devices, shards(): lax.all_gather(w_up, 'wide', axis=0, tiled=True)  101 us
    all_gather x1, waiting for transfers between devices, shards(): lax.all_gather(w_gate, 'wide', axis=0, tiled=True)  101 us
    unnamed x2, blocking collectives  85.6 us
  transfers between devices with their start and end apart: 16, of which 15 were waited for; matrix products, arithmetic and copies ran while one was open for 8% of the time, Pallas kernels for 0%

commit v1 on v0

--- a/solution.py
+++ b/solution.py
@@ -84,9 +84,26 @@
         lax.all_gather(norm1_gain, ("wide", "narrow"), axis=0, tiled=True),
         lax.all_gather(norm2_gain, ("wide", "narrow"), axis=0, tiled=True),
     )
+
+    def vectors_post(sheet, shard_axis, on_dim):
+        passed = lax.axis_size(shard_axis)
+        extra = lax.axis_index(shard_axis)
+        tile_out, local_part, z_new = (passed, extra, sheet.shape[on_dim])
+        gallery = [(hop_no, (hop_no + 1) % tile_out) for hop_no in range(tile_out)]
+        val = jnp.zeros(
+            (*sheet.shape[:on_dim], tile_out * z_new, *sheet.shape[on_dim + 1 :]), sheet.dtype
+        )
+        w2 = sheet
+        for at in range(tile_out):
+            current_value = (local_part - at) % tile_out
+            val = lax.dynamic_update_slice_in_dim(val, w2, current_value * z_new, axis=on_dim)
+            if at < tile_out - 1:
+                w2 = lax.ppermute(w2, axis_name=shard_axis, perm=gallery)
+        return val
+
     wgate_full, wup_full, wdown_full = (
         lax.all_gather(w_gate, "wide", axis=0, tiled=True),
-        lax.all_gather(w_up, "wide", axis=0, tiled=True),
+        vectors_post(w_up, "wide", 0),
         lax.all_gather(w_down, "wide", axis=1, tiled=True),
     )
     gain_one = gain_one.astype(jnp.float32)

time: 1380 us -> 1450 us (1.051)
  waiting for transfers between devices: 1090 us -> 1140 us
  local copies, waits for them, and re-layouts: 23.7 us -> 41.5 us
    ppermute x0 -> x7, waiting for transfers between devices: none -> 243 us  [vectors_post(): w2 = lax.ppermute(w2, axis_name=shard_axis, perm=gallery)]
    all_gather x1, waiting for transfers between devices: 111 us -> 0.01 us  [shards(): lax.all_gather(w_down, 'wide', axis=1, tiled=True)]
    all_gather x1, waiting for transfers between devices: 101 us -> 52.1 us  [shards(): lax.all_gather(w_gate, 'wide', axis=0, tiled=True)]
    all_gather x1, waiting for transfers between devices: 101 us -> 78.1 us  [shards(): lax.all_gather(w_up, 'wide', axis=0, tiled=True)]
  transfers between devices with their start and end apart: 16 -> 23, of which waited for: 15 -> 20; matrix products, arithmetic and copies ran while one was open for 8% -> 10% of each run, Pallas kernels for 0% -> 0%
where the time goes in v1:
time: 1450 us; the launch traced here: 1440 us
  waiting for transfers between devices  1140 us (79%)
  matrix products  124 us (9%)
  blocking collectives  97.3 us (7%)
  local copies, waits for them, and re-layouts  41.5 us (3%)
  other arithmetic  22 us (2%)
  between operations  14.7 us (1%)
    ppermute x7, waiting for transfers between devices, vectors_post(): w2 = lax.ppermute(w2, axis_name=shard_axis, perm=gallery)  243 us
    reduce_scatter x1, waiting for transfers between devices, shards(): lax.psum_scatter(grad_wqkv, ('wide', 'narrow'), scatter_dimension=0, tile...  160 us
    reduce_scatter x1, waiting for transfers between devices, shards(): lax.psum_scatter(grad_wout, ('wide', 'narrow'), scatter_dimension=1, tile...  139 us
    reduce_scatter x1, waiting for transfers between devices, shards(): lax.psum_scatter(grad_wup.astype(jnp.bfloat16), 'wide', scatter_dimension...  130 us
    reduce_scatter x1, waiting for transfers between devices, shards(): lax.psum_scatter(grad_wdown.astype(jnp.bfloat16), 'wide', scatter_dimensi...  129 us
    unnamed x2, blocking collectives  85.5 us
    all_gather x1, waiting for transfers between devices, shards(): lax.all_gather(w_up, 'wide', axis=0, tiled=True)  78.1 us
    reduce_scatter x1, waiting for transfers between devices, shards(): lax.psum_scatter(grad_wgate.astype(jnp.bfloat16), 'wide', scatter_dimensi...  75 us
  transfers between devices with their start and end apart: 23, of which 20 were waited for; matrix products, arithmetic and copies ran while one was open for 10% of the time, Pallas kernels for 0%

profile of v1, /device:TPU:0, one launch (start us, length us, event | category | flops | bytes accessed | tf_op | source)
XLA Modules:
  0.0 1441.9 jit_solution(9255937782083285823)
XLA Ops:
  13.2 42.4 %all-reduce.11 = (bf16[2048]{0:T(1024)(128)(2,1)S(1)}, bf16[1536]{0:T(1024)(128)(2,1)S(1)}, bf16[1536]{0:T(1024)(128)(2,1)S(1)}) all-reduce(bf16[2048]{0:T(1024)(128)(2,1)S(1)} %dynamic-update-slice.1, bf16[1536]{0:T(1024)(128)(2,1)S(1)} %dynamic-update-slice, ...), channel_id=1, replica_groups=mesh['wide'=8,'narrow'=4] {'wide','narrow'}, use_global_device_ids=true, to_apply=%add.5 | all-reduce | flops 5120 | bytes 20480
  58.8 24.0 %all-gather.9.cloned.1.call-done = bf16[1536,2048]{1,0:T(8,128)(2,1)} async-done(((bf16[48,2048]{1,0:T(8,128)(2,1)}), bf16[1536,2048]{1,0:T(8,128)(2,1)}) %all-gather.9.cloned.1.call-update) | async-done | bytes 6291472 | tf_op jit(solution)/shard_map/all_gather | solution.py:81
  109.2 38.7 %all-gather.11.cloned.1.call-done = bf16[1536,1536]{0,1:T(8,128)(2,1)} async-done(((bf16[1536,48]{0,1:T(8,128)(2,1)}), bf16[1536,1536]{0,1:T(8,128)(2,1)}) %all-gather.11.cloned.1.call-update) | async-done | bytes 4718608 | tf_op jit(solution)/shard_map/all_gather | solution.py:83
  156.4 23.2 %collective-permute-done = bf16[192,2240]{1,0:T(8,128)(2,1)S(1)} collective-permute-done((bf16[192,2240]{1,0:T(8,128)(2,1)}, bf16[192,2240]{1,0:T(8,128)(2,1)S(1)}, u32[]{:S(2)}, u32[]{:S(2)}) %collective-permute-start) | collective-permute-done | bytes 860192 | tf_op jit(solution)/shard_map/ppermute | solution.py:101
  180.5 43.7 %collective-permute-done.1 = bf16[192,2240]{1,0:T(8,128)(2,1)S(1)} collective-permute-done((bf16[192,2240]{1,0:T(8,128)(2,1)S(1)}, bf16[192,2240]{1,0:T(8,128)(2,1)S(1)}, u32[]{:S(2)}, u32[]{:S(2)}) %collective-permute-start.1) | collective-permute-done | bytes 860192 | tf_op jit(solution)/shard_map/ppermute | solution.py:101
  225.1 34.1 %collective-permute-done.2 = bf16[192,2240]{1,0:T(8,128)(2,1)S(1)} collective-permute-done((bf16[192,2240]{1,0:T(8,128)(2,1)S(1)}, bf16[192,2240]{1,0:T(8,128)(2,1)S(1)}, u32[]{:S(2)}, u32[]{:S(2)}) %collective-permute-start.2) | collective-permute-done | bytes 860192 | tf_op jit(solution)/shard_map/ppermute | solution.py:101
  260.1 43.3 %collective-permute-done.3 = bf16[192,2240]{1,0:T(8,128)(2,1)} collective-permute-done((bf16[192,2240]{1,0:T(8,128)(2,1)S(1)}, bf16[192,2240]{1,0:T(8,128)(2,1)}, u32[]{:S(2)}, u32[]{:S(2)}) %collective-permute-start.3) | collective-permute-done | bytes 860192 | tf_op jit(solution)/shard_map/ppermute | solution.py:101
  307.8 37.1 %collective-permute-done.4 = bf16[192,2240]{1,0:T(8,128)(2,1)} collective-permute-done((bf16[192,2240]{1,0:T(8,128)(2,1)}, bf16[192,2240]{1,0:T(8,128)(2,1)}, u32[]{:S(2)}, u32[]{:S(2)}) %collective-permute-start.4) | collective-permute-done | bytes 860192 | tf_op jit(solution)/shard_map/ppermute | solution.py:101
  347.8 32.2 %collective-permute-done.5 = bf16[192,2240]{1,0:T(8,128)(2,1)S(1)} collective-permute-done((bf16[192,2240]{1,0:T(8,128)(2,1)}, bf16[192,2240]{1,0:T(8,128)(2,1)S(1)}, u32[]{:S(2)}, u32[]{:S(2)}) %collective-permute-start.5) | collective-permute-done | bytes 860192 | tf_op jit(solution)/shard_map/ppermute | solution.py:101
  385.6 29.2 %collective-permute-done.6 = bf16[192,2240]{1,0:T(8,128)(2,1)S(1)} collective-permute-done((bf16[192,2240]{1,0:T(8,128)(2,1)S(1)}, bf16[192,2240]{1,0:T(8,128)(2,1)S(1)}, u32[]{:S(2)}, u32[]{:S(2)}) %collective-permute-start.6) | collective-permute-done | bytes 860192 | tf_op jit(solution)/shard_map/ppermute | solution.py:101
  425.2 52.1 %all-gather.15.cloned.1.call-done = bf16[1536,2240]{1,0:T(8,128)(2,1)} async-done(((bf16[192,2240]{1,0:T(8,128)(2,1)}), bf16[1536,2240]{1,0:T(8,128)(2,1)}) %all-gather.15.cloned.1.call-update) | async-done | bytes 6881296 | tf_op jit(solution)/shard_map/all_gather | solution.py:105
  477.3 19.8 %all-gather.13.cloned.1.call-done = bf16[512,1536]{1,0:T(8,128)(2,1)} async-done(((bf16[128,1536]{1,0:T(8,128)(2,1)}), bf16[512,1536]{1,0:T(8,128)(2,1)}) %all-gather.13.cloned.1.call-update) | async-done | bytes 1572880 | tf_op jit(solution)/shard_map/all_gather | solution.py:200
  497.2 9.6 fusion.47
  506.8 13.6 multiply_convert_fusion
  529.6 78.1 %all-gather.19.cloned.1.call-done = bf16[1536,2240]{1,0:T(8,128)(2,1)} async-done(((bf16[192,2240]{1,0:T(8,128)(2,1)}), bf16[1536,2240]{1,0:T(8,128)(2,1)}) %all-gather.19.cloned.1.call-update) | async-done | bytes 6881296 | tf_op jit(solution)/shard_map/all_gather | solution.py:215
  607.7 9.6 fusion.3
  626.8 16.9 %reduce-scatter.16.cloned.1.call-done = bf16[128,1536]{1,0:T(8,128)(2,1)} async-done(((bf16[512,1536]{1,0:T(8,128)(2,1)}), bf16[128,1536]{1,0:T(8,128)(2,1)}) %reduce-scatter.16.cloned.1.call-update) | async-done | bytes 393232 | tf_op jit(solution)/shard_map/reduce_scatter | solution.py:228
  646.9 27.9 %reduce-scatter.14.cloned.1.call-done = bf16[128,1536]{1,0:T(8,128)(2,1)} async-done(((bf16[512,1536]{1,0:T(8,128)(2,1)}), bf16[128,1536]{1,0:T(8,128)(2,1)}) %reduce-scatter.14.cloned.1.call-update) | async-done | bytes 393232 | tf_op jit(solution)/shard_map/reduce_scatter | solution.py:206
  748.4 43.1 %all-reduce.10 = (f32[2048]{0:T(1024)S(1)}, f32[1536]{0:T(1024)S(1)}, f32[1536]{0:T(1024)S(1)}) all-reduce(f32[2048]{0:T(1024)S(1)} %convert_reduce_fusion, f32[1536]{0:T(1024)S(1)} %get-tuple-element.83, f32[1536]{0:T(1024)S(1)} %copy-done.28), channel_id=8, replica_groups=mesh['wide'=8,'narrow'=4] {'wide','narrow'}, use_global_device_ids=true, to_apply=%region_16.17.clone | all-reduce | flops 5120 | bytes 40960
  794.4 75.0 %reduce-scatter.22.cloned.1.call-done = bf16[192,2240]{1,0:T(8,128)(2,1)} async-done(((bf16[1536,2240]{1,0:T(8,128)(2,1)}), bf16[192,2240]{1,0:T(8,128)(2,1)}) %reduce-scatter.22.cloned.1.call-update) | async-done | bytes 860176 | tf_op jit(solution)/shard_map/reduce_scatter | solution.py:322
  871.9 129.5 %reduce-scatter.24.cloned.1.call-done = bf16[192,2240]{1,0:T(8,128)(2,1)} async-done(((bf16[1536,2240]{1,0:T(8,128)(2,1)}), bf16[192,2240]{1,0:T(8,128)(2,1)}) %reduce-scatter.24.cloned.1.call-update) | async-done | bytes 860176 | tf_op jit(solution)/shard_map/reduce_scatter | solution.py:325
  1003.8 129.4 %reduce-scatter.26.cloned.1.call-done = bf16[2240,192]{0,1:T(8,128)(2,1)} async-done(((bf16[2240,1536]{0,1:T(8,128)(2,1)}), bf16[2240,192]{0,1:T(8,128)(2,1)}) %reduce-scatter.26.cloned.1.call-update) | async-done | bytes 860176 | tf_op jit(solution)/shard_map/reduce_scatter | solution.py:328
  1135.7 139.2 %reduce-scatter.20.cloned.1.call-done = f32[1536,48]{0,1:T(8,128)} async-done(((f32[1536,1536]{0,1:T(8,128)}), f32[1536,48]{0,1:T(8,128)}) %reduce-scatter.20.cloned.1.call-update) | async-done | bytes 294928 | tf_op jit(solution)/shard_map/reduce_scatter | solution.py:317
  1274.9 160.2 %reduce-scatter.18.cloned.1.call-done = f32[48,2048]{1,0:T(8,128)} async-done(((f32[1536,2048]{1,0:T(8,128)}), f32[48,2048]{1,0:T(8,128)}) %reduce-scatter.18.cloned.1.call-update) | async-done | bytes 393232 | tf_op jit(solution)/shard_map/reduce_scatter | solution.py:315
  (224 shorter events, 175.3 us)
Async XLA Ops:
  7.2 50.7 %copy-start.3 = (bf16[1,128,1536]{2,1,0:T(8,128)(2,1)S(1)}, bf16[1,128,1536]{2,1,0:T(8,128)(2,1)}, u32[]{:S(2)}) copy-start(bf16[1,128,1536]{2,1,0:T(8,128)(2,1)} %param.11) | copy-start | bytes 1179652
  7.2 75.6 %all-gather.9.cloned.1.call-start = ((), (), s32[]{:S(2)}) async-start(), calls=%async_computation.9 | async-start | bytes 6488064 | tf_op jit(solution)/shard_map/all_gather | solution.py:81
  7.9 140.0 %all-gather.11.cloned.1.call-start = ((), (), s32[]{:S(2)}) async-start(), calls=%async_computation.10 | async-start | bytes 4866048 | tf_op jit(solution)/shard_map/all_gather | solution.py:83
  8.7 407.1 %all-gather.21.cloned.1.call-start = ((), (), s32[]{:S(2)}) async-start(), calls=%async_computation.22 | async-start | bytes 1966080 | tf_op jit(solution)/shard_map/all_gather | solution.py:219
  9.4 406.3 %all-gather.17.cloned.1.call-start = ((), (), s32[]{:S(2)}) async-start(), calls=%async_computation.13 | async-start | bytes 7962624 | tf_op jit(solution)/shard_map/all_gather | solution.py:107
  10.0 467.4 %all-gather.15.cloned.1.call-start = ((), (), s32[]{:S(2)}) async-start(), calls=%async_computation.12 | async-start | bytes 7962624 | tf_op jit(solution)/shard_map/all_gather | solution.py:105
  10.6 486.6 %all-gather.13.cloned.1.call-start = ((), (), s32[]{:S(2)}) async-start(), calls=%async_computation.11 | async-start | bytes 1966080 | tf_op jit(solution)/shard_map/all_gather | solution.py:200
  154.0 453.6 %all-gather.19.cloned.1.call-start = ((), (), s32[]{:S(2)}) async-start(), calls=%async_computation.15 | async-start | bytes 7962624 | tf_op jit(solution)/shard_map/all_gather | solution.py:215
  154.8 488.9 %reduce-scatter.16.cloned.1.call-start = ((), (), s32[]{:S(2)}) async-start(), calls=%async_computation.16 | async-start | bytes 1966080 | tf_op jit(solution)/shard_map/reduce_scatter | solution.py:228
  154.8 24.8 %collective-permute-start = (bf16[192,2240]{1,0:T(8,128)(2,1)}, bf16[192,2240]{1,0:T(8,128)(2,1)S(1)}, u32[]{:S(2)}, u32[]{:S(2)}) collective-permute-start(bf16[192,2240]{1,0:T(8,128)(2,1)} %param.19), channel_id=1, source_target_pairs={{0,4},{4,8},{8,12},{12,16},{16,20},{20,24},{24,28},{28,0},{1,5},{5... | collective-permute-start | bytes 2580488 | tf_op jit(solution)/shard_map/ppermute | solution.py:101
  180.5 43.7 %collective-permute-start.1 = (bf16[192,2240]{1,0:T(8,128)(2,1)S(1)}, bf16[192,2240]{1,0:T(8,128)(2,1)S(1)}, u32[]{:S(2)}, u32[]{:S(2)}) collective-permute-start(bf16[192,2240]{1,0:T(8,128)(2,1)S(1)} %collective-permute-done), channel_id=1, source_target_pairs={{0,4},{4,8},{8,12},{12,16},{16,20},{20,24},{24,28},{28,0},{1,5},{5... | collective-permute-start | bytes 2580488 | tf_op jit(solution)/shard_map/ppermute | solution.py:101
  225.1 34.1 %collective-permute-start.2 = (bf16[192,2240]{1,0:T(8,128)(2,1)S(1)}, bf16[192,2240]{1,0:T(8,128)(2,1)S(1)}, u32[]{:S(2)}, u32[]{:S(2)}) collective-permute-start(bf16[192,2240]{1,0:T(8,128)(2,1)S(1)} %collective-permute-done.1), channel_id=1, source_target_pairs={{0,4},{4,8},{8,12},{12,16},{16,20},{20,24},{24,28},{28,0},{1,5},{5... | collective-permute-start | bytes 2580488 | tf_op jit(solution)/shard_map/ppermute | solution.py:101
  260.1 43.3 %collective-permute-start.3 = (bf16[192,2240]{1,0:T(8,128)(2,1)S(1)}, bf16[192,2240]{1,0:T(8,128)(2,1)}, u32[]{:S(2)}, u32[]{:S(2)}) collective-permute-start(bf16[192,2240]{1,0:T(8,128)(2,1)S(1)} %collective-permute-done.2), channel_id=1, source_target_pairs={{0,4},{4,8},{8,12},{12,16},{16,20},{20,24},{24,28},{28,0},{1,5},{5... | collective-permute-start | bytes 2580488 | tf_op jit(solution)/shard_map/ppermute | solution.py:101
  303.4 41.5 %collective-permute-start.4 = (bf16[192,2240]{1,0:T(8,128)(2,1)}, bf16[192,2240]{1,0:T(8,128)(2,1)}, u32[]{:S(2)}, u32[]{:S(2)}) collective-permute-start(bf16[192,2240]{1,0:T(8,128)(2,1)} %collective-permute-done.3), channel_id=1, source_target_pairs={{0,4},{4,8},{8,12},{12,16},{16,20},{20,24},{24,28},{28,0},{1,5},{5... | collective-permute-start | bytes 2580488 | tf_op jit(solution)/shard_map/ppermute | solution.py:101
  344.9 35.1 %collective-permute-start.5 = (bf16[192,2240]{1,0:T(8,128)(2,1)}, bf16[192,2240]{1,0:T(8,128)(2,1)S(1)}, u32[]{:S(2)}, u32[]{:S(2)}) collective-permute-start(bf16[192,2240]{1,0:T(8,128)(2,1)} %collective-permute-done.4), channel_id=1, source_target_pairs={{0,4},{4,8},{8,12},{12,16},{16,20},{20,24},{24,28},{28,0},{1,5},{5... | collective-permute-start | bytes 2580488 | tf_op jit(solution)/shard_map/ppermute | solution.py:101
  380.0 34.7 %collective-permute-start.6 = (bf16[192,2240]{1,0:T(8,128)(2,1)S(1)}, bf16[192,2240]{1,0:T(8,128)(2,1)S(1)}, u32[]{:S(2)}, u32[]{:S(2)}) collective-permute-start(bf16[192,2240]{1,0:T(8,128)(2,1)S(1)} %collective-permute-done.5), channel_id=1, source_target_pairs={{0,4},{4,8},{8,12},{12,16},{16,20},{20,24},{24,28},{28,0},{1,5},{5... | collective-permute-start | bytes 2580488 | tf_op jit(solution)/shard_map/ppermute | solution.py:101
  617.3 57.5 %reduce-scatter.14.cloned.1.call-start = ((), (), s32[]{:S(2)}) async-start(), calls=%async_computation.14 | async-start | bytes 1966080 | tf_op jit(solution)/shard_map/reduce_scatter | solution.py:206
  626.7 105.2 %reduce-scatter.28.cloned.1.call-start = ((), (), s32[]{:S(2)}) async-start(), calls=%async_computation.23 | async-start | bytes 327680
  692.2 43.4 %reduce-scatter.30.cloned.1.call-start = ((), (), s32[]{:S(2)}) async-start(), calls=%async_computation.24 | async-start | bytes 327680
  696.7 172.6 %reduce-scatter.22.cloned.1.call-start = ((), (), s32[]{:S(2)}) async-start(), calls=%async_computation.19 | async-start | bytes 7962624 | tf_op jit(solution)/shard_map/reduce_scatter | solution.py:322
  705.7 295.6 %reduce-scatter.24.cloned.1.call-start = ((), (), s32[]{:S(2)}) async-start(), calls=%async_computation.20 | async-start | bytes 7962624 | tf_op jit(solution)/shard_map/reduce_scatter | solution.py:325
  714.7 418.5 %reduce-scatter.26.cloned.1.call-start = ((), (), s32[]{:S(2)}) async-start(), calls=%async_computation.21 | async-start | bytes 7962624 | tf_op jit(solution)/shard_map/reduce_scatter | solution.py:328
  723.6 551.3 %reduce-scatter.20.cloned.1.call-start = ((), (), s32[]{:S(2)}) async-start(), calls=%async_computation.18 | async-start | bytes 9732096 | tf_op jit(solution)/shard_map/reduce_scatter | solution.py:317
  729.9 705.2 %reduce-scatter.18.cloned.1.call-start = ((), (), s32[]{:S(2)}) async-start(), calls=%async_computation.17 | async-start | bytes 12976128 | tf_op jit(solution)/shard_map/reduce_scatter | solution.py:315
  (40 other events, 422.0 us)
Sparse Core Ops, SparseCore 0:
  10.9 71.9 all-gather.8
  85.7 62.1 all-gather.10
  149.5 17.9 all-gather.20
  169.5 157.7 all-gather.16
  329.3 147.9 all-gather.14
  479.3 17.7 all-gather.12
  499.4 108.2 all-gather.18
  617.4 26.2 reduce-scatter.15
  646.8 27.9 reduce-scatter.13
  692.3 20.0 reduce-scatter.27
  715.5 20.0 reduce-scatter.29
  739.1 130.2 reduce-scatter.21
  873.0 128.2 reduce-scatter.23
  1004.9 128.2 reduce-scatter.25
  1139.5 135.3 reduce-scatter.19
  1281.4 153.7 reduce-scatter.17
